TPU v7x, 256 devices: a whole 4x4x8 slice. The times are simulated.
256 devices in a mesh: dp: 4 (over x), ep: 64 (over y, z, core).
Axes of the slice: x: 4, y: 4, z: 8, core: 2. Of those that a mesh axis runs over, the one named last changes fastest.
Arguments:
- tokens: bfloat16 [2048, 3584], P(('dp', 'ep')), may hold values from -6 to 6
- expert_ids: int32 [2, 2048, 8], P(None, ('dp', 'ep')), may hold values from 0 to 63, all different within a row; in each aligned block of 8 rows (0 to 7, 8 to 15, ..., all dimensions but the last counted through in order) at most 2 rows name the same one
- quant_gates: int32 [2, 2048, 8], P(None, ('dp', 'ep')), may hold values from 1 to 63
- w_gate: bfloat16 [2, 64, 3584, 1024], P(None, 'ep', None, 'dp'), may hold values from -0.09375 to 0.09375
- w_up: bfloat16 [2, 64, 3584, 1024], P(None, 'ep', None, 'dp'), may hold values from -0.09375 to 0.09375
- w_down: bfloat16 [2, 64, 1024, 3584], P(None, 'ep', 'dp'), may hold values from -0.1875 to 0.1875
Outputs:
- stream_out: bfloat16 [2048, 3584], P(('dp', 'ep'))
- expert_load: int32 [2, 64], replicated
Inputs may be any that keep to these rules, and one draw needn't show every extreme that they name: `expert_ids`: in each layer, the 8 tokens of one device name any one expert at most 2 times, a bound that some block reaches.
All inputs are finite; a program needn't handle non-finite values.
Results may differ from a plain program's by a relative error of at most 0.015.
Values may be sent and summed in bfloat16 or wider, within the bound.
No kernel may reach another device: no remote copies, remote signals or barrier semaphores. Data moves between devices by JAX's collectives and lax.ppermute only.
A program may use at most 64 MiB of HBM per device.

v0:
```python
import functools

import jax
import jax.numpy as jnp
from jax import lax
from jax.experimental import pallas as pl
from jax.experimental.pallas import tpu as pltpu
from jax.sharding import Mesh
from jax.sharding import PartitionSpec as P


EP = ("ep_0", "ep_1", "ep_2")
DP_EP = ("dp", "ep_0", "ep_1", "ep_2")

ROUTE_SCALE = 2.827
EPS = 1e-06
BF16 = jnp.bfloat16
F32 = jnp.float32
LANES = 128
CHUNK = 512
ROWS = 256
GRANT = 20 * 1024 * 1024
STEPS = (0, -1, 1, 2)


def shift(array, step):
    n_dp = lax.axis_size("dp")
    return lax.ppermute(array, "dp", [(i, (i + step) % n_dp) for i in range(n_dp)])


def ring_gather(own, dim):
    half = own.shape[dim] // 2
    left, right = shift(own, 1), shift(own, -1)
    first = shift(lax.slice_in_dim(left, 0, half, axis=dim), 1)
    second = shift(lax.slice_in_dim(right, half, 2 * half, axis=dim), -1)
    return own, left, right, first, second


def exchange(piece_for):
    got = []
    for step in STEPS:
        got.append(shift(piece_for(-step), -step) if step else piece_for(0))
    return got


def place_blocks(blocks, dim):
    n_dp = lax.axis_size("dp")
    shape = list(blocks[0].shape)
    length = shape[dim]
    shape[dim] *= n_dp
    out = jnp.zeros(shape, blocks[0].dtype)
    for step, block in zip(STEPS, blocks):
        start = ((lax.axis_index("dp") + step) % n_dp) * length
        out = lax.dynamic_update_slice_in_dim(out, block, start, axis=dim)
    return out


def dot(a, b):
    return jnp.dot(a, b, preferred_element_type=F32)


def silu_times(gate, upper):
    return gate / (1.0 + jnp.exp(-gate)) * upper


def vmem(count):
    return [pl.BlockSpec(memory_space=pltpu.VMEM)] * count


def loop(count):
    return pl.loop(0, count)


def rows_at(index, size):
    return pl.ds(pl.multiple_of(index * size, size), size)


def hbm(count):
    return [pl.BlockSpec(memory_space=pltpu.HBM)] * count


def hidden_kernel(layer, *refs):
    pieces, (gate_ref, up_ref, out_ref, gate_sum, up_sum) = refs[:-5], refs[-5:]
    gate_sum[...] = jnp.zeros_like(gate_sum)
    up_sum[...] = jnp.zeros_like(up_sum)
    start = 0
    for piece in pieces:

        @loop(piece.shape[1] // ROWS)
        def _(i):
            rows = piece[:, rows_at(i, ROWS)]
            at = pl.ds(pl.multiple_of(start + i * ROWS, ROWS), ROWS)
            gate_sum[...] += dot(rows, gate_ref[layer, 0, at, :])
            up_sum[...] += dot(rows, up_ref[layer, 0, at, :])

        start += piece.shape[1]
    out_ref[...] = silu_times(gate_sum[...], up_sum[...]).astype(out_ref.dtype)


def hidden_units(pieces, w_gate, w_up, layer):
    rows = pieces[0].shape[0]
    _, _, width, units = w_gate.shape
    return pl.pallas_call(
        functools.partial(hidden_kernel, layer),
        out_shape=jax.ShapeDtypeStruct((rows, units), BF16),
        in_specs=vmem(len(pieces) + 2),
        out_specs=vmem(1)[0],
        scratch_shapes=[pltpu.VMEM((rows, units), F32)] * 2,
        cost_estimate=pl.CostEstimate(
            flops=4 * rows * units * width, bytes_accessed=4 * units * width, transcendentals=rows * units
        ),
        compiler_params=pltpu.CompilerParams(vmem_limit_bytes=GRANT),
        name="hidden_units",
    )(*pieces, w_gate, w_up)


def down_kernel(*refs):
    count = len(STEPS)
    hidden, weights, out_ref = refs[:count], refs[count : 2 * count], refs[2 * count]

    @loop(out_ref.shape[0] // ROWS)
    def _(i):
        at = rows_at(i, ROWS)
        total = dot(hidden[0][at, :], weights[0][...])
        for hidden_ref, weight_ref in zip(hidden[1:], weights[1:]):
            total = total + dot(hidden_ref[at, :], weight_ref[...])
        out_ref[at, :] = total.astype(out_ref.dtype)


def down(hidden, weights):
    rows, units = hidden[0].shape
    part = weights[0].shape[1]
    return pl.pallas_call(
        down_kernel,
        out_shape=jax.ShapeDtypeStruct((rows, part), BF16),
        in_specs=vmem(2 * len(hidden)),
        out_specs=vmem(1)[0],
        cost_estimate=pl.CostEstimate(
            flops=2 * rows * units * part * len(hidden), bytes_accessed=2 * units * part * len(hidden), transcendentals=0
        ),
        compiler_params=pltpu.CompilerParams(vmem_limit_bytes=GRANT),
        name="down",
    )(*hidden, *weights)


def two_parts(value):
    high = value.astype(BF16)
    low = (value - high.astype(F32)).astype(BF16)
    lane = lax.broadcasted_iota(jnp.int32, (value.shape[0], LANES), 1)
    wide = jnp.where(lane == 0, high.astype(F32), jnp.where(lane == 1, low.astype(F32), 0.0))
    return wide.astype(BF16)


def one_value(parts):
    return jnp.sum(parts.astype(F32), axis=1, keepdims=True)


def spread_place(row, me, slots, capacity):
    n_dp = len(STEPS)
    place = row // slots
    away = jnp.where(place == 0, 0, jnp.where(place == 1, n_dp - 1, jnp.where(place == 2, 1, 2)))
    slot = row % slots
    return ((slot // capacity) * n_dp + (me + away) % n_dp) * capacity + slot % capacity


def partial_kernel(capacity, starts_ref, rows_ref, *refs):
    sources, (out_ref, arrived, sorted_ref, held, done) = refs[:-5], refs[-5:]
    count, _, units = held.shape
    total = sorted_ref.shape[0]
    first = pltpu.make_async_copy(rows_ref, arrived, done.at[count])
    copies = [pltpu.make_async_copy(source, held.at[k], done.at[k]) for k, source in enumerate(sources)]
    first.start()
    for copy in copies:
        copy.start()
    first.wait()

    @loop(total // ROWS)
    def _(i):
        at = rows_at(i, ROWS)
        row = lax.broadcasted_iota(jnp.int32, (ROWS, total), 0) + i * ROWS
        wanted = spread_place(row, starts_ref[count], total // len(STEPS), capacity)
        order = (wanted == lax.broadcasted_iota(jnp.int32, (ROWS, total), 1)).astype(F32).astype(BF16)
        rows = dot(order, arrived[...])
        sorted_ref[at, :] = rows.astype(BF16)
        out_ref[at, count * units :] = two_parts(jnp.sum(rows * rows, axis=1, keepdims=True))

    for copy in copies:
        copy.wait()

    @loop(count)
    def _(k):
        start = pl.multiple_of(starts_ref[k], units)
        out_ref[:, pl.ds(start, units)] = dot(sorted_ref[...], held[k]).astype(BF16)


def partial_products(me, rows, capacity, gates, ups):
    count, part = rows.shape
    n_dp = len(STEPS)
    units = gates[0].shape[1]
    weights = [weight for pair in zip(gates, ups) for weight in pair]
    starts = jnp.stack([(2 * ((me + step) % n_dp) + k) * units for step in STEPS for k in range(2)] + [me])
    return pl.pallas_call(
        functools.partial(partial_kernel, capacity),
        out_shape=jax.ShapeDtypeStruct((count, len(weights) * units + LANES), BF16),
        in_specs=[pl.BlockSpec(memory_space=pltpu.SMEM)] + hbm(1 + len(weights)),
        out_specs=vmem(1)[0],
        scratch_shapes=[
            pltpu.VMEM((count, part), BF16),
            pltpu.VMEM((count, part), BF16),
            pltpu.VMEM((len(weights), part, units), BF16),
            pltpu.SemaphoreType.DMA((len(weights) + 1,)),
        ],
        cost_estimate=pl.CostEstimate(
            flops=2 * count * part * (len(weights) * units + count), bytes_accessed=4 * n_dp * part * units, transcendentals=0
        ),
        compiler_params=pltpu.CompilerParams(vmem_limit_bytes=GRANT),
        name="partial_products",
    )(starts, rows, *weights)


def fold_kernel(left_ref, right_ref, from_left_ref, from_right_ref, left_out, right_out):
    half = from_left_ref.shape[0]
    last = left_ref.shape[1] - LANES
    for ref, arrived, out, at, other in (
        (right_ref, from_left_ref, right_out, slice(0, half), slice(half, 2 * half)),
        (left_ref, from_right_ref, left_out, slice(half, 2 * half), slice(0, half)),
    ):
        out[other, :] = ref[other, :]
        out[at, :last] = (ref[at, :last].astype(F32) + arrived[:, :last].astype(F32)).astype(BF16)
        out[at, last:] = two_parts(one_value(ref[at, last:]) + one_value(arrived[:, last:]))


def fold(products, from_left, from_right):
    height, width = products.shape[0] // len(STEPS), products.shape[1]
    return pl.pallas_call(
        fold_kernel,
        out_shape=[jax.ShapeDtypeStruct((height, width), BF16)] * 2,
        grid=(1,),
        in_specs=[pl.BlockSpec((height, width), lambda i: (1, 0)), pl.BlockSpec((height, width), lambda i: (2, 0))] + vmem(2),
        out_specs=vmem(2),
        cost_estimate=pl.CostEstimate(flops=height * width * 8, bytes_accessed=height * width * 8, transcendentals=0),
        compiler_params=pltpu.CompilerParams(vmem_limit_bytes=GRANT),
        name="fold",
    )(products, products, from_left, from_right)


def finish_kernel(layer, me_ref, products, left_ref, right_ref, w0, w1, w2, w3, w4, out_ref, hidden_ref, own_ref, held, done):
    n_dp = len(STEPS)
    units = w1.shape[0]
    half = units // 2
    width = out_ref.shape[1]
    last = own_ref.shape[1] - LANES
    first = pltpu.make_async_copy(products.at[: own_ref.shape[0]], own_ref, done.at[5])
    first.start()
    targets = [held.at[i] for i in range(3)] + [held.at[3, :half], held.at[3, half:]]
    copies = [
        pltpu.make_async_copy(source, target, done.at[k])
        for k, (source, target) in enumerate(zip((w0.at[layer, 0], w1, w2, w3, w4), targets))
    ]
    for copy in copies:
        copy.start()
    first.wait()

    def total(start, size):
        at = slice(start, start + size)
        return own_ref[:, at].astype(F32) + left_ref[:, at].astype(F32) + right_ref[:, at].astype(F32)

    square = one_value(own_ref[:, last:]) + one_value(left_ref[:, last:]) + one_value(right_ref[:, last:])
    scale = lax.rsqrt(square / width + EPS)
    for i in range(n_dp):
        gate = total(2 * i * units, units) * scale
        upper = total((2 * i + 1) * units, units) * scale
        hidden_ref[:, i * units : (i + 1) * units] = silu_times(gate, upper).astype(BF16)
    for copy in copies:
        copy.wait()

    def block(step):
        at = pl.multiple_of(((me_ref[0] + step + n_dp) % n_dp) * units, units)
        return hidden_ref[:, pl.ds(at, units)]

    @loop(width // CHUNK)
    def _(i):
        at = rows_at(i, CHUNK)
        result = dot(block(STEPS[0]), held[0, :, at])
        for k in range(1, n_dp):
            result = result + dot(block(STEPS[k]), held[k, :, at])
        out_ref[:, at] = result.astype(BF16)


def finish(me, products, left, right, w_down, layer, others):
    rows = left.shape[0]
    _, _, units, width = w_down.shape
    n_dp = len(STEPS)
    return pl.pallas_call(
        functools.partial(finish_kernel, layer),
        out_shape=jax.ShapeDtypeStruct((rows, width), BF16),
        in_specs=[pl.BlockSpec(memory_space=pltpu.SMEM)] + hbm(1) + vmem(2) + hbm(1 + len(others)),
        out_specs=vmem(1)[0],
        scratch_shapes=[
            pltpu.VMEM((rows, n_dp * units), BF16),
            pltpu.VMEM(left.shape, BF16),
            pltpu.VMEM((n_dp, units, width), BF16),
            pltpu.SemaphoreType.DMA((2 + len(others),)),
        ],
        cost_estimate=pl.CostEstimate(
            flops=2 * rows * n_dp * units * width, bytes_accessed=2 * n_dp * units * width, transcendentals=rows * n_dp * units
        ),
        compiler_params=pltpu.CompilerParams(vmem_limit_bytes=GRANT),
        name="finish",
    )(me, products, left, right, w_down, *others)


def slot_picks(ids, experts, capacity, lines):
    rows, top = ids.shape
    tokens = rows // lines
    expert_iota = lax.broadcasted_iota(jnp.int32, (lines, tokens * top, experts), 2)
    onehot = (ids.reshape(lines, tokens * top)[:, :, None] == expert_iota).astype(F32)
    before = jnp.tril(jnp.ones((tokens * top, tokens * top), F32), -1)
    earlier = jnp.einsum("ab,lbe->lae", before, onehot, preferred_element_type=F32)
    place = jnp.sum(earlier * onehot, axis=2).astype(jnp.int32).reshape(rows, top)
    line = lax.broadcasted_iota(jnp.int32, (rows, top), 0) // tokens
    target = (ids * lines + line) * capacity + place
    slot_iota = lax.broadcasted_iota(jnp.int32, (rows, top, experts * lines * capacity), 2)
    return target[:, :, None] == slot_iota


def gates_of(quant):
    wide = quant.astype(F32)
    return ROUTE_SCALE * wide / jnp.sum(wide, axis=1, keepdims=True)


def spread_of(picked, quant):
    return jnp.sum(jnp.where(picked, gates_of(quant)[:, :, None], 0.0), axis=1)


def chosen_of(picked):
    return jnp.any(picked, axis=1).astype(BF16)


def swap(rows):
    return lax.all_to_all(rows, EP, split_axis=0, concat_axis=0, tiled=True)


def weighted(spread, rows):
    return jnp.dot(spread, rows.astype(F32), precision=lax.Precision.HIGHEST, preferred_element_type=F32)


def per_device(tokens, expert_ids, quant_gates, w_gate, w_up, w_down):
    layers, count_tok, top = expert_ids.shape
    n_dp = lax.axis_size("dp")
    n_ep = lax.axis_size(EP)
    me = lax.axis_index("dp").astype(jnp.int32)
    me_vector = me.reshape(1)
    capacity = min(count_tok, max(2, 3 * count_tok * top // (2 * n_ep)))
    width = tokens.shape[1]
    units = w_gate.shape[3]
    part = width // n_dp
    slots = n_ep * capacity
    count = n_dp * slots

    def around(step, size):
        return ((me + step) % n_dp) * size

    wide = tokens.astype(F32)
    normed = (wide * lax.rsqrt(jnp.mean(wide * wide, axis=1, keepdims=True) + EPS)).astype(BF16)
    own_picks = [slot_picks(expert_ids[i], n_ep, capacity, 1) for i in range(layers)]
    arrived = swap(dot(chosen_of(own_picks[0]).T, normed).astype(BF16))

    down_slices = exchange(
        lambda step: lax.dynamic_slice(w_down, (0, 0, 0, around(step, part)), (1, 1, units, part))[0, 0]
    )
    routes = jnp.concatenate([*expert_ids, *quant_gates], axis=1).astype(BF16)
    routes = jnp.pad(routes, ((0, 0), (0, LANES - routes.shape[1])))
    line = exchange(
        lambda step: jnp.concatenate(
            [lax.dynamic_slice_in_dim(tokens, around(step, part), part, axis=1), routes], axis=1
        ),
    )
    line = place_blocks(line, 0)
    state = line[:, :part]
    routes = line[:, part:].astype(jnp.int32)
    line_ids = [routes[:, i * top : (i + 1) * top] for i in range(layers)]
    line_quant = [routes[:, (layers + i) * top : (layers + i + 1) * top] for i in range(layers)]
    line_picks = [slot_picks(ids, n_ep, capacity, n_dp) for ids in line_ids]
    expert_iota = lax.broadcasted_iota(jnp.int32, (1, 1, n_ep), 2)
    loads = jnp.stack([jnp.sum((ids[:, :, None] == expert_iota).astype(jnp.int32), axis=(0, 1)) for ids in line_ids])
    for axis in EP:
        loads = lax.psum(loads, axis)

    def rows_of(weight):
        return lambda step: lax.dynamic_slice(weight, (1, 0, around(step, part), 0), (1, 1, part, units))[0, 0]

    gates = exchange(rows_of(w_gate))
    ups = exchange(rows_of(w_up))
    whole_down = ring_gather(w_down[1, 0], 0)[1:]

    own, left, right, first, second = ring_gather(arrived, 1)
    hidden = []
    for block in (own, left, right):
        hidden.append(hidden_units([block], w_gate, w_up, 0))
    block = jnp.concatenate([first, second], axis=1)
    hidden.append(silu_times(dot(block, w_gate[0, 0]), dot(block, w_up[0, 0])).astype(BF16))
    hidden = jnp.concatenate(hidden, axis=0)
    out_row = lax.broadcasted_iota(jnp.int32, (count, count), 0)
    in_row = lax.broadcasted_iota(jnp.int32, (count, count), 1)
    moved = out_row == spread_place(in_row, me, slots, capacity)
    hidden = dot(moved.astype(BF16), hidden).astype(BF16)
    blocks = exchange(lambda step: hidden)
    returned = swap(down(blocks, down_slices))
    branch = weighted(spread_of(line_picks[0], line_quant[0]), returned)
    state = (state.astype(F32) + branch).astype(BF16)

    arrived = swap(dot(chosen_of(line_picks[1]).T, state).astype(BF16))
    own_rows = exchange(lambda step: lax.dynamic_slice_in_dim(state, around(step, count_tok), count_tok, axis=0))
    own_rows = place_blocks(own_rows, 1)
    products = partial_products(me, arrived, capacity, gates, ups)
    middle = count - slots // 2
    from_left, from_right = shift(products[count - slots : middle], 1), shift(products[middle:], -1)
    left, right = fold(products, from_left, from_right)
    from_left, from_right = shift(right, 1), shift(left, -1)
    message = finish(me_vector, products, from_left, from_right, w_down, 1, whole_down)
    returned = swap(message)
    branch = weighted(spread_of(own_picks[1], quant_gates[1]), returned)
    stream_out = (own_rows.astype(F32) + branch).astype(BF16)
    return (stream_out, loads)


def solution(mesh):
    finer = Mesh(mesh.devices.reshape(mesh.shape["dp"], 4, 8, 2), DP_EP)
    placed = (
        P(DP_EP, None),
        P(None, DP_EP, None),
        P(None, DP_EP, None),
        P(None, EP, None, "dp"),
        P(None, EP, None, "dp"),
        P(None, EP, "dp", None),
    )

    return jax.shard_map(per_device, mesh=finer, in_specs=placed, out_specs=(P(DP_EP, None), P()), check_vma=False)
```

profile of v0, /device:TPU:1, one launch (start us, length us, event | category | flops | bytes accessed | tf_op | source)
XLA Modules:
  0.0 296.8 jit_solution(13588216477899851982)
XLA Ops:
  6.7 13.1 %all-to-all-start = ((bf16[64,2,3584]{2,1,0:T(2,128)(2,1)}), bf16[64,2,3584]{2,1,0:T(2,128)(2,1)S(1)}, u32[]{:S(2)}, u32[]{:S(2)}) async-start(bf16[64,2,3584]{2,1,0:T(2,128)(2,1)} %all_to_all.30), calls=%async_computation | async-start | bytes 1835008 | tf_op jit(solution)/shard_map/all_to_all | solution.py:341
  26.9 18.7 %all-to-all-done = bf16[64,2,3584]{2,1,0:T(2,128)(2,1)S(1)} async-done(((bf16[64,2,3584]{2,1,0:T(2,128)(2,1)}), bf16[64,2,3584]{2,1,0:T(2,128)(2,1)S(1)}, u32[]{:S(2)}, u32[]{:S(2)}) %all-to-all-start) | async-done | bytes 917536 | tf_op jit(solution)/shard_map/all_to_all | solution.py:341
  48.5 2.8 slice_bitcast_fusion
  51.3 19.7 %collective-permute-done.3.refs_0_ = bf16[128,3584]{1,0:T(8,128)(2,1)S(1)} collective-permute-done((bf16[128,3584]{1,0:T(8,128)(2,1)S(1)}, bf16[128,3584]{1,0:T(8,128)(2,1)S(1)}, u32[]{:S(2)}, u32[]{:S(2)}) %collective-permute-start.3) | collective-permute-done | bytes 917536 | tf_op jit(solution)/shard_map/ppermute | solution.py:28
  76.6 2.7 hidden_units.3
  79.3 2.7 hidden_units.5
  82.1 2.7 hidden_units.4
  93.8 5.2 %collective-permute-done.8.refs_2_ = bf16[512,256]{1,0:T(8,128)(2,1)} collective-permute-done((bf16[512,256]{1,0:T(8,128)(2,1)S(1)}, bf16[512,256]{1,0:T(8,128)(2,1)}, u32[]{:S(2)}, u32[]{:S(2)}) %collective-permute-start.8) | collective-permute-done | bytes 262176 | tf_op jit(solution)/shard_map/ppermute | solution.py:28
  102.5 3.6 %down.1 = bf16[512,896]{1,0:T(8,128)(2,1)} custom-call(bf16[512,256]{1,0:T(8,128)(2,1)S(1)} %convolution_convert_fusion.2.refs_0_, bf16[512,256]{1,0:T(8,128)(2,1)} %collective-permute-done.7.refs_1_, bf16[512,256]{1,0:T(8,128)(2,1)} %collective-permute-done.8.refs_2_, bf16[512,256]{1,0:T(8,128)(2,1)} %collective-permute-done.9.refs_3_, ...), custom_call_target="tpu_custom_call" | custom-call | flops 939524096 | bytes 1835008 | tf_op jit(solution)/shard_map/down/pallas_call | solution.py:133
  106.1 10.8 %all-to-all-start.1 = ((bf16[64,8,896]{2,1,0:T(8,128)(2,1)}), bf16[64,8,896]{2,1,0:T(8,128)(2,1)S(1)}, u32[]{:S(2)}, u32[]{:S(2)}) async-start(bf16[64,8,896]{2,1,0:T(8,128)(2,1)} %bitcast.14), calls=%async_computation.1 | async-start | bytes 1835008 | tf_op jit(solution)/shard_map/all_to_all | solution.py:341
  117.0 24.1 %collective-permute-done = bf16[8,1024]{1,0:T(8,128)(2,1)} collective-permute-done((bf16[8,1024]{1,0:T(8,128)(2,1)}, bf16[8,1024]{1,0:T(8,128)(2,1)}, u32[]{:S(2)}, u32[]{:S(2)}) %collective-permute-start) | collective-permute-done | bytes 16416 | tf_op jit(solution)/shard_map/ppermute | solution.py:28
  146.9 7.2 %all-to-all-start.2 = ((bf16[64,8,896]{2,1,0:T(8,128)(2,1)}), bf16[64,8,896]{2,1,0:T(8,128)(2,1)S(1)}, u32[]{:S(2)}, u32[]{:S(2)}) async-start(bf16[64,8,896]{2,1,0:T(8,128)(2,1)} %fusion.6), calls=%async_computation.2 | async-start | bytes 1835008 | tf_op jit(solution)/shard_map/all_to_all | solution.py:341
  161.4 8.6 %collective-permute-done.20.refs_6_ = bf16[896,256]{1,0:T(8,128)(2,1)S(1)} collective-permute-done((bf16[896,256]{1,0:T(8,128)(2,1)S(1)}, bf16[896,256]{1,0:T(8,128)(2,1)S(1)}, u32[]{:S(2)}, u32[]{:S(2)}) %collective-permute-start.20) | collective-permute-done | bytes 458784 | tf_op jit(solution)/shard_map/ppermute | solution.py:28
  177.2 4.2 %collective-permute-done.16.refs_2_ = bf16[896,256]{1,0:T(8,128)(2,1)} collective-permute-done((bf16[896,256]{1,0:T(8,128)(2,1)}, bf16[896,256]{1,0:T(8,128)(2,1)}, u32[]{:S(2)}, u32[]{:S(2)}) %collective-permute-start.16) | collective-permute-done | bytes 458784 | tf_op jit(solution)/shard_map/ppermute | solution.py:28
  182.9 6.9 %collective-permute-done.21.refs_7_ = bf16[896,256]{1,0:T(8,128)(2,1)} collective-permute-done((bf16[896,256]{1,0:T(8,128)(2,1)}, bf16[896,256]{1,0:T(8,128)(2,1)}, u32[]{:S(2)}, u32[]{:S(2)}) %collective-permute-start.21) | collective-permute-done | bytes 458784 | tf_op jit(solution)/shard_map/ppermute | solution.py:28
  189.8 10.6 %collective-permute-done.17.refs_3_ = bf16[896,256]{1,0:T(8,128)(2,1)} collective-permute-done((bf16[896,256]{1,0:T(8,128)(2,1)}, bf16[896,256]{1,0:T(8,128)(2,1)}, u32[]{:S(2)}, u32[]{:S(2)}) %collective-permute-start.17) | collective-permute-done | bytes 458784 | tf_op jit(solution)/shard_map/ppermute | solution.py:28
  202.4 6.7 %partial_products.1.left_ref.right_ref.products = bf16[512,2176]{1,0:T(8,128)(2,1)S(1)} custom-call(s32[9]{0:T(128)S(1)} %stack.45.starts_ref, bf16[512,896]{1,0:T(8,128)(2,1)S(1)} %bitcast.106, bf16[896,256]{1,0:T(8,128)(2,1)S(1)} %get-tuple-element.12.refs_0_, bf16[896,256]{1,0:T(8,128)(2,1)S(1)} %copy-done.4, ...), custom_call_target="tpu_custom_call" | custom-call | flops 2348810240 | bytes 3670016 | tf_op jit(solution)/shard_map/partial_products/pallas_call | solution.py:202
  210.7 12.6 %collective-permute-done.23.from_right_ref = bf16[64,2176]{1,0:T(8,128)(2,1)S(1)} collective-permute-done((bf16[64,2176]{1,0:T(8,128)(2,1)S(1)}, bf16[64,2176]{1,0:T(8,128)(2,1)S(1)}, u32[]{:S(2)}, u32[]{:S(2)}) %collective-permute-start.23) | collective-permute-done | bytes 278560 | tf_op jit(solution)/shard_map/ppermute | solution.py:28
  229.0 12.2 %collective-permute-done.24.left_ref = bf16[128,2176]{1,0:T(8,128)(2,1)S(1)} collective-permute-done((bf16[128,2176]{1,0:T(8,128)(2,1)S(1)}, bf16[128,2176]{1,0:T(8,128)(2,1)S(1)}, u32[]{:S(2)}, u32[]{:S(2)}) %collective-permute-start.24) | collective-permute-done | bytes 557088 | tf_op jit(solution)/shard_map/ppermute | solution.py:28
  241.2 4.5 %finish.1 = bf16[128,3584]{1,0:T(8,128)(2,1)S(1)} custom-call(s32[1]{0:T(128)} %bitcast.19.me_ref, bf16[512,2176]{1,0:T(8,128)(2,1)S(1)} %partial_products.1.left_ref.right_ref.products, bf16[128,2176]{1,0:T(8,128)(2,1)S(1)} %collective-permute-done.24.left_ref, bf16[128,2176]{1,0:T(8,128)(2,1)S(1)} %collective-permute-done.25.right_ref, ...), custom_call_target="tpu_custom_call" | custom-call | flops 939524096 | bytes 7340032 | tf_op jit(solution)/shard_map/finish/pallas_call | solution.py:294
  247.0 11.3 %all-to-all-start.3 = ((bf16[64,2,3584]{2,1,0:T(2,128)(2,1)}), bf16[64,2,3584]{2,1,0:T(2,128)(2,1)S(1)}, u32[]{:S(2)}, u32[]{:S(2)}) async-start(bf16[64,2,3584]{2,1,0:T(2,128)(2,1)} %all_to_all.39), calls=%async_computation.3 | async-start | bytes 1835008 | tf_op jit(solution)/shard_map/all_to_all | solution.py:341
  258.9 7.7 %psum.21 = s32[2,64]{1,0:T(2,128)S(1)} all-reduce(s32[2,64]{1,0:T(2,128)S(1)} %pad_add_fusion), channel_id=1, replica_groups=mesh['dp'=4,'ep_0'=4,'ep_1'=8,'ep_2'=2] {'ep_0'}, use_global_device_ids=true, to_apply=%region_13.14 | all-reduce | flops 128 | bytes 1024 | tf_op jit(solution)/shard_map/psum | solution.py:388
  266.6 20.0 %psum.22 = s32[2,64]{1,0:T(2,128)S(1)} all-reduce(s32[2,64]{1,0:T(2,128)S(1)} %psum.21), channel_id=1, replica_groups=mesh['dp'=4,'ep_0'=4,'ep_1'=8,'ep_2'=2] {'ep_1'}, use_global_device_ids=true, to_apply=%region_14.15 | all-reduce | flops 128 | bytes 1024 | tf_op jit(solution)/shard_map/psum | solution.py:388
  286.6 3.9 %psum.23 = s32[2,64]{1,0:T(2,128)} all-reduce(s32[2,64]{1,0:T(2,128)S(1)} %psum.22), channel_id=1, replica_groups=mesh['dp'=4,'ep_0'=4,'ep_1'=8,'ep_2'=2] {'ep_2'}, use_global_device_ids=true, to_apply=%region_15.16 | all-reduce | flops 128 | bytes 1024 | tf_op jit(solution)/shard_map/psum | solution.py:388
  (159 shorter events, 72.8 us)
Async XLA Ops:
  6.7 38.9 %all-to-all-start = ((bf16[64,2,3584]{2,1,0:T(2,128)(2,1)}), bf16[64,2,3584]{2,1,0:T(2,128)(2,1)S(1)}, u32[]{:S(2)}, u32[]{:S(2)}) async-start(bf16[64,2,3584]{2,1,0:T(2,128)(2,1)} %all_to_all.30), calls=%async_computation | async-start | bytes 1835008 | tf_op jit(solution)/shard_map/all_to_all | solution.py:341
  22.6 65.0 %collective-permute-start.12 = (bf16[256,896]{1,0:T(8,128)(2,1)}, bf16[256,896]{1,0:T(8,128)(2,1)S(1)}, u32[]{:S(2)}, u32[]{:S(2)}) collective-permute-start(bf16[256,896]{1,0:T(8,128)(2,1)} %get-tuple-element.14), channel_id=1, source_target_pairs={{0,128},{64,192},{128,0},{192,64},{1,129},{65,193},{129,1},{193,65... | collective-permute-start | bytes 1376264 | tf_op jit(solution)/shard_map/ppermute | solution.py:28
  25.3 63.9 %collective-permute-start.11 = (bf16[256,896]{1,0:T(8,128)(2,1)}, bf16[256,896]{1,0:T(8,128)(2,1)S(1)}, u32[]{:S(2)}, u32[]{:S(2)}) collective-permute-start(bf16[256,896]{1,0:T(8,128)(2,1)} %get-tuple-element.15), channel_id=1, source_target_pairs={{0,192},{64,0},{128,64},{192,128},{1,193},{65,1},{129,65},{193,129... | collective-permute-start | bytes 1376264 | tf_op jit(solution)/shard_map/ppermute | solution.py:28
  26.2 65.2 %collective-permute-start.10 = (bf16[256,896]{1,0:T(8,128)(2,1)}, bf16[256,896]{1,0:T(8,128)(2,1)}, u32[]{:S(2)}, u32[]{:S(2)}) collective-permute-start(bf16[256,896]{1,0:T(8,128)(2,1)} %get-tuple-element.16), channel_id=1, source_target_pairs={{0,64},{64,128},{128,192},{192,0},{1,65},{65,129},{129,193},{193,1... | collective-permute-start | bytes 1376264 | tf_op jit(solution)/shard_map/ppermute | solution.py:28
  45.9 25.8 %collective-permute-start.4 = (bf16[128,3584]{1,0:T(8,128)(2,1)S(1)}, bf16[128,3584]{1,0:T(8,128)(2,1)S(1)}, u32[]{:S(2)}, u32[]{:S(2)}) collective-permute-start(bf16[128,3584]{1,0:T(8,128)(2,1)S(1)} %all_to_all.32.refs_0_), channel_id=1, source_target_pairs={{0,192},{64,0},{128,64},{192,128},{1,193},{65,1},{129,65},{193,129... | collective-permute-start | bytes 2752520 | tf_op jit(solution)/shard_map/ppermute | solution.py:28
  48.5 22.6 %collective-permute-start.3 = (bf16[128,3584]{1,0:T(8,128)(2,1)S(1)}, bf16[128,3584]{1,0:T(8,128)(2,1)S(1)}, u32[]{:S(2)}, u32[]{:S(2)}) collective-permute-start(bf16[128,3584]{1,0:T(8,128)(2,1)S(1)} %all_to_all.32.refs_0_), channel_id=1, source_target_pairs={{0,64},{64,128},{128,192},{192,0},{1,65},{65,129},{129,193},{193,1... | collective-permute-start | bytes 2752520 | tf_op jit(solution)/shard_map/ppermute | solution.py:28
  89.2 82.1 %collective-permute-start.27 = (bf16[256,3584]{1,0:T(8,128)(2,1)}, bf16[256,3584]{1,0:T(8,128)(2,1)S(1)}, u32[]{:S(2)}, u32[]{:S(2)}) collective-permute-start(bf16[256,3584]{1,0:T(8,128)(2,1)} %slice_bitcast_fusion), channel_id=1, source_target_pairs={{0,192},{64,0},{128,64},{192,128},{1,193},{65,1},{129,65},{193,129... | collective-permute-start | bytes 5505032 | tf_op jit(solution)/shard_map/ppermute | solution.py:28
  91.4 80.5 %collective-permute-start.26 = (bf16[256,3584]{1,0:T(8,128)(2,1)}, bf16[256,3584]{1,0:T(8,128)(2,1)}, u32[]{:S(2)}, u32[]{:S(2)}) collective-permute-start(bf16[256,3584]{1,0:T(8,128)(2,1)} %slice_bitcast_fusion), channel_id=1, source_target_pairs={{0,64},{64,128},{128,192},{192,0},{1,65},{65,129},{129,193},{193,1... | collective-permute-start | bytes 5505032 | tf_op jit(solution)/shard_map/ppermute | solution.py:28
  93.8 48.7 %collective-permute-start.2 = (bf16[8,1024]{1,0:T(8,128)(2,1)}, bf16[8,1024]{1,0:T(8,128)(2,1)}, u32[]{:S(2)}, u32[]{:S(2)}) collective-permute-start(bf16[8,1024]{1,0:T(8,128)(2,1)} %get-tuple-element.40), channel_id=1, source_target_pairs={{0,128},{64,192},{128,0},{192,64},{1,129},{65,193},{129,1},{193,65... | collective-permute-start | bytes 49160 | tf_op jit(solution)/shard_map/ppermute | solution.py:28
  99.0 42.1 %collective-permute-start = (bf16[8,1024]{1,0:T(8,128)(2,1)}, bf16[8,1024]{1,0:T(8,128)(2,1)}, u32[]{:S(2)}, u32[]{:S(2)}) collective-permute-start(bf16[8,1024]{1,0:T(8,128)(2,1)} %get-tuple-element.41), channel_id=1, source_target_pairs={{0,64},{64,128},{128,192},{192,0},{1,65},{65,129},{129,193},{193,1... | collective-permute-start | bytes 49160 | tf_op jit(solution)/shard_map/ppermute | solution.py:28
  101.2 40.6 %collective-permute-start.1 = (bf16[8,1024]{1,0:T(8,128)(2,1)}, bf16[8,1024]{1,0:T(8,128)(2,1)}, u32[]{:S(2)}, u32[]{:S(2)}) collective-permute-start(bf16[8,1024]{1,0:T(8,128)(2,1)} %get-tuple-element.42), channel_id=1, source_target_pairs={{0,192},{64,0},{128,64},{192,128},{1,193},{65,1},{129,65},{193,129... | collective-permute-start | bytes 49160 | tf_op jit(solution)/shard_map/ppermute | solution.py:28
  106.1 38.9 %all-to-all-start.1 = ((bf16[64,8,896]{2,1,0:T(8,128)(2,1)}), bf16[64,8,896]{2,1,0:T(8,128)(2,1)S(1)}, u32[]{:S(2)}, u32[]{:S(2)}) async-start(bf16[64,8,896]{2,1,0:T(8,128)(2,1)} %bitcast.14), calls=%async_computation.1 | async-start | bytes 1835008 | tf_op jit(solution)/shard_map/all_to_all | solution.py:341
  146.9 53.4 %all-to-all-start.2 = ((bf16[64,8,896]{2,1,0:T(8,128)(2,1)}), bf16[64,8,896]{2,1,0:T(8,128)(2,1)S(1)}, u32[]{:S(2)}, u32[]{:S(2)}) async-start(bf16[64,8,896]{2,1,0:T(8,128)(2,1)} %fusion.6), calls=%async_computation.2 | async-start | bytes 1835008 | tf_op jit(solution)/shard_map/all_to_all | solution.py:341
  157.4 24.1 %collective-permute-start.16 = (bf16[896,256]{1,0:T(8,128)(2,1)}, bf16[896,256]{1,0:T(8,128)(2,1)}, u32[]{:S(2)}, u32[]{:S(2)}) collective-permute-start(bf16[896,256]{1,0:T(8,128)(2,1)} %get-tuple-element.11), channel_id=1, source_target_pairs={{0,64},{64,128},{128,192},{192,0},{1,65},{65,129},{129,193},{193,1... | collective-permute-start | bytes 1376264 | tf_op jit(solution)/shard_map/ppermute | solution.py:28
  158.0 23.5 %collective-permute-start.18 = (bf16[896,256]{1,0:T(8,128)(2,1)}, bf16[896,256]{1,0:T(8,128)(2,1)}, u32[]{:S(2)}, u32[]{:S(2)}) collective-permute-start(bf16[896,256]{1,0:T(8,128)(2,1)} %get-tuple-element.13), channel_id=1, source_target_pairs={{0,192},{64,0},{128,64},{192,128},{1,193},{65,1},{129,65},{193,129... | collective-permute-start | bytes 1376264 | tf_op jit(solution)/shard_map/ppermute | solution.py:28
  170.8 19.0 %collective-permute-start.21 = (bf16[896,256]{1,0:T(8,128)(2,1)}, bf16[896,256]{1,0:T(8,128)(2,1)}, u32[]{:S(2)}, u32[]{:S(2)}) collective-permute-start(bf16[896,256]{1,0:T(8,128)(2,1)} %get-tuple-element.6), channel_id=1, source_target_pairs={{0,128},{64,192},{128,0},{192,64},{1,129},{65,193},{129,1},{193,65... | collective-permute-start | bytes 1376264 | tf_op jit(solution)/shard_map/ppermute | solution.py:28
  171.3 29.0 %collective-permute-start.17 = (bf16[896,256]{1,0:T(8,128)(2,1)}, bf16[896,256]{1,0:T(8,128)(2,1)}, u32[]{:S(2)}, u32[]{:S(2)}) collective-permute-start(bf16[896,256]{1,0:T(8,128)(2,1)} %get-tuple-element.7), channel_id=1, source_target_pairs={{0,64},{64,128},{128,192},{192,0},{1,65},{65,129},{129,193},{193,1... | collective-permute-start | bytes 1376264 | tf_op jit(solution)/shard_map/ppermute | solution.py:28
  171.9 28.5 %collective-permute-start.19 = (bf16[896,256]{1,0:T(8,128)(2,1)}, bf16[896,256]{1,0:T(8,128)(2,1)}, u32[]{:S(2)}, u32[]{:S(2)}) collective-permute-start(bf16[896,256]{1,0:T(8,128)(2,1)} %get-tuple-element.9), channel_id=1, source_target_pairs={{0,192},{64,0},{128,64},{192,128},{1,193},{65,1},{129,65},{193,129... | collective-permute-start | bytes 1376264 | tf_op jit(solution)/shard_map/ppermute | solution.py:28
  181.5 47.5 %collective-permute-start.29 = (bf16[128,3584]{1,0:T(8,128)(2,1)}, bf16[128,3584]{1,0:T(8,128)(2,1)}, u32[]{:S(2)}, u32[]{:S(2)}) collective-permute-start(bf16[128,3584]{1,0:T(8,128)(2,1)} %slice.69), channel_id=1, source_target_pairs={{0,192},{64,0},{128,64},{192,128},{1,193},{65,1},{129,65},{193,129... | collective-permute-start | bytes 2752520 | tf_op jit(solution)/shard_map/ppermute | solution.py:28
  181.5 47.5 %collective-permute-start.28 = (bf16[128,3584]{1,0:T(8,128)(2,1)}, bf16[128,3584]{1,0:T(8,128)(2,1)}, u32[]{:S(2)}, u32[]{:S(2)}) collective-permute-start(bf16[128,3584]{1,0:T(8,128)(2,1)} %slice.68), channel_id=1, source_target_pairs={{0,64},{64,128},{128,192},{192,0},{1,65},{65,129},{129,193},{193,1... | collective-permute-start | bytes 2752520 | tf_op jit(solution)/shard_map/ppermute | solution.py:28
  209.8 16.1 %collective-permute-start.22 = (bf16[64,2176]{1,0:T(8,128)(2,1)S(1)}, bf16[64,2176]{1,0:T(8,128)(2,1)S(1)}, u32[]{:S(2)}, u32[]{:S(2)}) collective-permute-start(bf16[64,2176]{1,0:T(8,128)(2,1)S(1)} %get-tuple-element.19), channel_id=1, source_target_pairs={{0,64},{64,128},{128,192},{192,0},{1,65},{65,129},{129,193},{193,1... | collective-permute-start | bytes 835592 | tf_op jit(solution)/shard_map/ppermute | solution.py:28
  226.2 15.0 %collective-permute-start.24 = (bf16[128,2176]{1,0:T(8,128)(2,1)S(1)}, bf16[128,2176]{1,0:T(8,128)(2,1)S(1)}, u32[]{:S(2)}, u32[]{:S(2)}) collective-permute-start(bf16[128,2176]{1,0:T(8,128)(2,1)S(1)} %get-tuple-element.4), channel_id=1, source_target_pairs={{0,64},{64,128},{128,192},{192,0},{1,65},{65,129},{129,193},{193,1... | collective-permute-start | bytes 1671176 | tf_op jit(solution)/shard_map/ppermute | solution.py:28
  247.0 48.3 %all-to-all-start.3 = ((bf16[64,2,3584]{2,1,0:T(2,128)(2,1)}), bf16[64,2,3584]{2,1,0:T(2,128)(2,1)S(1)}, u32[]{:S(2)}, u32[]{:S(2)}) async-start(bf16[64,2,3584]{2,1,0:T(2,128)(2,1)} %all_to_all.39), calls=%async_computation.3 | async-start | bytes 1835008 | tf_op jit(solution)/shard_map/all_to_all | solution.py:341
  258.8 34.4 %collective-permute-start.13 = (bf16[8,896]{1,0:T(8,128)(2,1)S(1)}, bf16[8,896]{1,0:T(8,128)(2,1)S(1)}, u32[]{:S(2)}, u32[]{:S(2)}) collective-permute-start(bf16[8,896]{1,0:T(8,128)(2,1)S(1)} %get-tuple-element.22), channel_id=1, source_target_pairs={{0,64},{64,128},{128,192},{192,0},{1,65},{65,129},{129,193},{193,1... | collective-permute-start | bytes 43016 | tf_op jit(solution)/shard_map/ppermute | solution.py:28
  (24 other events, 351.2 us)
where the time goes:
time: 298 us; the launch traced here: 297 us
  waiting for transfers between devices  131 us (44%)
  starting transfers between devices  73.1 us (25%)
  blocking collectives  31.6 us (11%)
  local copies, waits for them, and re-layouts  23.9 us (8%)
  Pallas kernels  23.4 us (8%)
  matrix products  6.49 us (2%)
  other arithmetic  5.66 us (2%)
    ppermute x30, waiting for transfers between devices, shift(): lax.ppermute(array, 'dp', [(i, (i + step) % n_dp) for i in range(n_dp)])  113 us
    all_to_all x4, starting transfers between devices, swap(): return lax.all_to_all(rows, EP, split_axis=0, concat_axis=0, tiled=True)  42.5 us
    psum x3, blocking collectives, per_device(): loads = lax.psum(loads, axis)  31.6 us
    ppermute x30, starting transfers between devices, shift(): lax.ppermute(array, 'dp', [(i, (i + step) % n_dp) for i in range(n_dp)])  30.6 us
    all_to_all x4, waiting for transfers between devices, swap(): return lax.all_to_all(rows, EP, split_axis=0, concat_axis=0, tiled=True)  18.7 us
    pallas_call x3, Pallas kernels, hidden_units(): pl.pallas_call(functools.partial(hidden_kernel, layer), out_shape=jax.Sha...  8.24 us
    pallas_call x1, Pallas kernels, partial_products(): pl.pallas_call(functools.partial(partial_kernel, capacity), out_shape=jax...  6.69 us
  transfers between devices with their start and end apart: 34, of which 14 were waited for; matrix products, arithmetic and copies ran while one was open for 7% of the time, Pallas kernels for 6%

commit v1 on v0

--- a/solution.py
+++ b/solution.py
@@ -79,7 +79,7 @@
     return [pl.BlockSpec(memory_space=pltpu.HBM)] * count
 
 
-def hidden_kernel(layer, *refs):
+def hidden_kernel(*refs):
     pieces, (gate_ref, up_ref, out_ref, gate_sum, up_sum) = refs[:-5], refs[-5:]
     gate_sum[...] = jnp.zeros_like(gate_sum)
     up_sum[...] = jnp.zeros_like(up_sum)
@@ -90,8 +90,8 @@
         def _(i):
             rows = piece[:, rows_at(i, ROWS)]
             at = pl.ds(pl.multiple_of(start + i * ROWS, ROWS), ROWS)
-            gate_sum[...] += dot(rows, gate_ref[layer, 0, at, :])
-            up_sum[...] += dot(rows, up_ref[layer, 0, at, :])
+            gate_sum[...] += dot(rows, gate_ref[0, 0, at, :])
+            up_sum[...] += dot(rows, up_ref[0, 0, at, :])
 
         start += piece.shape[1]
     out_ref[...] = silu_times(gate_sum[...], up_sum[...]).astype(out_ref.dtype)
@@ -101,15 +101,15 @@
     rows = pieces[0].shape[0]
     _, _, width, units = w_gate.shape
     return pl.pallas_call(
-        functools.partial(hidden_kernel, layer),
+        hidden_kernel,
         out_shape=jax.ShapeDtypeStruct((rows, units), BF16),
-        in_specs=vmem(len(pieces) + 2),
+        grid=(1,),
+        in_specs=vmem(len(pieces)) + [pl.BlockSpec((1, 1, width, units), lambda i: (layer, 0, 0, 0))] * 2,
         out_specs=vmem(1)[0],
         scratch_shapes=[pltpu.VMEM((rows, units), F32)] * 2,
         cost_estimate=pl.CostEstimate(
             flops=4 * rows * units * width, bytes_accessed=4 * units * width, transcendentals=rows * units
         ),
-        compiler_params=pltpu.CompilerParams(vmem_limit_bytes=GRANT),
         name="hidden_units",
     )(*pieces, w_gate, w_up)
 

time: 298 us -> 309 us (1.037)
  Pallas kernels: 23.4 us -> 32.2 us
    pallas_call x3, Pallas kernels: 8.24 us -> 17.1 us  [hidden_units(): pl.pallas_call(hidden_kernel, out_shape=jax.ShapeDtypeStruct((rows, units...]
  transfers between devices with their start and end apart: 34 -> 34, of which waited for: 14 -> 14; matrix products, arithmetic and copies ran while one was open for 7% -> 8% of each run, Pallas kernels for 6% -> 9%
where the time goes in v1:
time: 309 us; the launch traced here: 308 us
  waiting for transfers between devices  133 us (43%)
  starting transfers between devices  71.7 us (23%)
  Pallas kernels  32.2 us (10%)
  blocking collectives  31.6 us (10%)
  local copies, waits for them, and re-layouts  24.8 us (8%)
  matrix products  8.13 us (3%)
  other arithmetic  5.71 us (2%)
    ppermute x30, waiting for transfers between devices, shift(): lax.ppermute(array, 'dp', [(i, (i + step) % n_dp) for i in range(n_dp)])  114 us
    all_to_all x4, starting transfers between devices, swap(): return lax.all_to_all(rows, EP, split_axis=0, concat_axis=0, tiled=True)  40.5 us
    psum x3, blocking collectives, per_device(): loads = lax.psum(loads, axis)  31.6 us
    ppermute x30, starting transfers between devices, shift(): lax.ppermute(array, 'dp', [(i, (i + step) % n_dp) for i in range(n_dp)])  31.2 us
    all_to_all x4, waiting for transfers between devices, swap(): return lax.all_to_all(rows, EP, split_axis=0, concat_axis=0, tiled=True)  18.7 us
    pallas_call x3, Pallas kernels, hidden_units(): pl.pallas_call(hidden_kernel, out_shape=jax.ShapeDtypeStruct((rows, units...  17.1 us
    pallas_call x1, Pallas kernels, partial_products(): pl.pallas_call(functools.partial(partial_kernel, capacity), out_shape=jax...  6.69 us
  transfers between devices with their start and end apart: 34, of which 14 were waited for; matrix products, arithmetic and copies ran while one was open for 8% of the time, Pallas kernels for 9%

profile of v1, /device:TPU:1, one launch (start us, length us, event | category | flops | bytes accessed | tf_op | source)
XLA Modules:
  0.0 308.0 jit_solution(1633580318716807198)
XLA Ops:
  6.7 13.1 %all-to-all-start = ((bf16[64,2,3584]{2,1,0:T(2,128)(2,1)}), bf16[64,2,3584]{2,1,0:T(2,128)(2,1)S(1)}, u32[]{:S(2)}, u32[]{:S(2)}) async-start(bf16[64,2,3584]{2,1,0:T(2,128)(2,1)} %all_to_all.30), calls=%async_computation | async-start | bytes 1835008 | tf_op jit(solution)/shard_map/all_to_all | solution.py:341
  26.9 18.7 %all-to-all-done = bf16[64,2,3584]{2,1,0:T(2,128)(2,1)S(1)} async-done(((bf16[64,2,3584]{2,1,0:T(2,128)(2,1)}), bf16[64,2,3584]{2,1,0:T(2,128)(2,1)S(1)}, u32[]{:S(2)}, u32[]{:S(2)}) %all-to-all-start) | async-done | bytes 917536 | tf_op jit(solution)/shard_map/all_to_all | solution.py:341
  48.5 2.8 slice_bitcast_fusion
  51.3 19.7 %collective-permute-done.3.refs_0_ = bf16[128,3584]{1,0:T(8,128)(2,1)S(1)} collective-permute-done((bf16[128,3584]{1,0:T(8,128)(2,1)S(1)}, bf16[128,3584]{1,0:T(8,128)(2,1)S(1)}, u32[]{:S(2)}, u32[]{:S(2)}) %collective-permute-start.3) | collective-permute-done | bytes 917536 | tf_op jit(solution)/shard_map/ppermute | solution.py:28
  75.4 5.7 %hidden_units.3 = bf16[128,256]{1,0:T(8,128)(2,1)} custom-call(bf16[128,3584]{1,0:T(8,128)(2,1)} %copy-done.6, bf16[2,1,3584,256]{3,2,1,0:T(8,128)(2,1)} %refs_1_.5, bf16[2,1,3584,256]{3,2,1,0:T(8,128)(2,1)} %refs_2_.5), custom_call_target="tpu_custom_call" | custom-call | flops 469762048 | bytes 3670016 | tf_op jit(solution)/shard_map/hidden_units/pallas_call | solution.py:103
  81.0 5.7 %hidden_units.5 = bf16[128,256]{1,0:T(8,128)(2,1)} custom-call(bf16[128,3584]{1,0:T(8,128)(2,1)} %copy-done.7, bf16[2,1,3584,256]{3,2,1,0:T(8,128)(2,1)} %refs_1_.5, bf16[2,1,3584,256]{3,2,1,0:T(8,128)(2,1)} %refs_2_.5), custom_call_target="tpu_custom_call" | custom-call | flops 469762048 | bytes 3670016 | tf_op jit(solution)/shard_map/hidden_units/pallas_call | solution.py:103
  86.7 5.7 %hidden_units.4 = bf16[128,256]{1,0:T(8,128)(2,1)} custom-call(bf16[128,3584]{1,0:T(8,128)(2,1)} %copy-done.8, bf16[2,1,3584,256]{3,2,1,0:T(8,128)(2,1)} %refs_1_.5, bf16[2,1,3584,256]{3,2,1,0:T(8,128)(2,1)} %refs_2_.5), custom_call_target="tpu_custom_call" | custom-call | flops 469762048 | bytes 3670016 | tf_op jit(solution)/shard_map/hidden_units/pallas_call | solution.py:103
  105.2 4.3 %collective-permute-done.8.refs_2_ = bf16[512,256]{1,0:T(8,128)(2,1)} collective-permute-done((bf16[512,256]{1,0:T(8,128)(2,1)S(1)}, bf16[512,256]{1,0:T(8,128)(2,1)}, u32[]{:S(2)}, u32[]{:S(2)}) %collective-permute-start.8) | collective-permute-done | bytes 262176 | tf_op jit(solution)/shard_map/ppermute | solution.py:28
  113.1 3.6 %down.1 = bf16[512,896]{1,0:T(8,128)(2,1)} custom-call(bf16[512,256]{1,0:T(8,128)(2,1)S(1)} %convolution_convert_fusion.2.refs_0_, bf16[512,256]{1,0:T(8,128)(2,1)} %collective-permute-done.7.refs_1_, bf16[512,256]{1,0:T(8,128)(2,1)} %collective-permute-done.8.refs_2_, bf16[512,256]{1,0:T(8,128)(2,1)} %collective-permute-done.9.refs_3_, ...), custom_call_target="tpu_custom_call" | custom-call | flops 939524096 | bytes 1835008 | tf_op jit(solution)/shard_map/down/pallas_call | solution.py:133
  116.7 9.2 %all-to-all-start.1 = ((bf16[64,8,896]{2,1,0:T(8,128)(2,1)}), bf16[64,8,896]{2,1,0:T(8,128)(2,1)S(1)}, u32[]{:S(2)}, u32[]{:S(2)}) async-start(bf16[64,8,896]{2,1,0:T(8,128)(2,1)} %bitcast.14), calls=%async_computation.1 | async-start | bytes 1835008 | tf_op jit(solution)/shard_map/all_to_all | solution.py:341
  125.9 26.7 %collective-permute-done = bf16[8,1024]{1,0:T(8,128)(2,1)} collective-permute-done((bf16[8,1024]{1,0:T(8,128)(2,1)}, bf16[8,1024]{1,0:T(8,128)(2,1)}, u32[]{:S(2)}, u32[]{:S(2)}) %collective-permute-start) | collective-permute-done | bytes 16416 | tf_op jit(solution)/shard_map/ppermute | solution.py:28
  158.5 6.9 %all-to-all-start.2 = ((bf16[64,8,896]{2,1,0:T(8,128)(2,1)}), bf16[64,8,896]{2,1,0:T(8,128)(2,1)S(1)}, u32[]{:S(2)}, u32[]{:S(2)}) async-start(bf16[64,8,896]{2,1,0:T(8,128)(2,1)} %fusion.6), calls=%async_computation.2 | async-start | bytes 1835008 | tf_op jit(solution)/shard_map/all_to_all | solution.py:341
  172.6 8.6 %collective-permute-done.20.refs_6_ = bf16[896,256]{1,0:T(8,128)(2,1)S(1)} collective-permute-done((bf16[896,256]{1,0:T(8,128)(2,1)S(1)}, bf16[896,256]{1,0:T(8,128)(2,1)S(1)}, u32[]{:S(2)}, u32[]{:S(2)}) %collective-permute-start.20) | collective-permute-done | bytes 458784 | tf_op jit(solution)/shard_map/ppermute | solution.py:28
  188.5 4.2 %collective-permute-done.16.refs_2_ = bf16[896,256]{1,0:T(8,128)(2,1)} collective-permute-done((bf16[896,256]{1,0:T(8,128)(2,1)}, bf16[896,256]{1,0:T(8,128)(2,1)}, u32[]{:S(2)}, u32[]{:S(2)}) %collective-permute-start.16) | collective-permute-done | bytes 458784 | tf_op jit(solution)/shard_map/ppermute | solution.py:28
  194.1 6.9 %collective-permute-done.21.refs_7_ = bf16[896,256]{1,0:T(8,128)(2,1)} collective-permute-done((bf16[896,256]{1,0:T(8,128)(2,1)}, bf16[896,256]{1,0:T(8,128)(2,1)}, u32[]{:S(2)}, u32[]{:S(2)}) %collective-permute-start.21) | collective-permute-done | bytes 458784 | tf_op jit(solution)/shard_map/ppermute | solution.py:28
  201.0 10.6 %collective-permute-done.17.refs_3_ = bf16[896,256]{1,0:T(8,128)(2,1)} collective-permute-done((bf16[896,256]{1,0:T(8,128)(2,1)}, bf16[896,256]{1,0:T(8,128)(2,1)}, u32[]{:S(2)}, u32[]{:S(2)}) %collective-permute-start.17) | collective-permute-done | bytes 458784 | tf_op jit(solution)/shard_map/ppermute | solution.py:28
  213.6 6.7 %partial_products.1.left_ref.right_ref.products = bf16[512,2176]{1,0:T(8,128)(2,1)S(1)} custom-call(s32[9]{0:T(128)S(1)} %stack.45.starts_ref, bf16[512,896]{1,0:T(8,128)(2,1)S(1)} %bitcast.106, bf16[896,256]{1,0:T(8,128)(2,1)S(1)} %get-tuple-element.12.refs_0_, bf16[896,256]{1,0:T(8,128)(2,1)S(1)} %copy-done.1, ...), custom_call_target="tpu_custom_call" | custom-call | flops 2348810240 | bytes 3670016 | tf_op jit(solution)/shard_map/partial_products/pallas_call | solution.py:202
  221.9 12.4 %collective-permute-done.23.from_right_ref = bf16[64,2176]{1,0:T(8,128)(2,1)S(1)} collective-permute-done((bf16[64,2176]{1,0:T(8,128)(2,1)S(1)}, bf16[64,2176]{1,0:T(8,128)(2,1)S(1)}, u32[]{:S(2)}, u32[]{:S(2)}) %collective-permute-start.23) | collective-permute-done | bytes 278560 | tf_op jit(solution)/shard_map/ppermute | solution.py:28
  240.2 12.2 %collective-permute-done.24.left_ref = bf16[128,2176]{1,0:T(8,128)(2,1)S(1)} collective-permute-done((bf16[128,2176]{1,0:T(8,128)(2,1)S(1)}, bf16[128,2176]{1,0:T(8,128)(2,1)S(1)}, u32[]{:S(2)}, u32[]{:S(2)}) %collective-permute-start.24) | collective-permute-done | bytes 557088 | tf_op jit(solution)/shard_map/ppermute | solution.py:28
  252.4 4.5 %finish.1 = bf16[128,3584]{1,0:T(8,128)(2,1)S(1)} custom-call(s32[1]{0:T(128)} %bitcast.19.me_ref, bf16[512,2176]{1,0:T(8,128)(2,1)S(1)} %partial_products.1.left_ref.right_ref.products, bf16[128,2176]{1,0:T(8,128)(2,1)S(1)} %collective-permute-done.24.left_ref, bf16[128,2176]{1,0:T(8,128)(2,1)S(1)} %collective-permute-done.25.right_ref, ...), custom_call_target="tpu_custom_call" | custom-call | flops 939524096 | bytes 7340032 | tf_op jit(solution)/shard_map/finish/pallas_call | solution.py:294
  258.2 11.3 %all-to-all-start.3 = ((bf16[64,2,3584]{2,1,0:T(2,128)(2,1)}), bf16[64,2,3584]{2,1,0:T(2,128)(2,1)S(1)}, u32[]{:S(2)}, u32[]{:S(2)}) async-start(bf16[64,2,3584]{2,1,0:T(2,128)(2,1)} %all_to_all.39), calls=%async_computation.3 | async-start | bytes 1835008 | tf_op jit(solution)/shard_map/all_to_all | solution.py:341
  270.1 7.7 %psum.21 = s32[2,64]{1,0:T(2,128)S(1)} all-reduce(s32[2,64]{1,0:T(2,128)S(1)} %pad_add_fusion), channel_id=1, replica_groups=mesh['dp'=4,'ep_0'=4,'ep_1'=8,'ep_2'=2] {'ep_0'}, use_global_device_ids=true, to_apply=%region_13.14 | all-reduce | flops 128 | bytes 1024 | tf_op jit(solution)/shard_map/psum | solution.py:388
  277.8 20.0 %psum.22 = s32[2,64]{1,0:T(2,128)S(1)} all-reduce(s32[2,64]{1,0:T(2,128)S(1)} %psum.21), channel_id=1, replica_groups=mesh['dp'=4,'ep_0'=4,'ep_1'=8,'ep_2'=2] {'ep_1'}, use_global_device_ids=true, to_apply=%region_14.15 | all-reduce | flops 128 | bytes 1024 | tf_op jit(solution)/shard_map/psum | solution.py:388
  297.8 3.9 %psum.23 = s32[2,64]{1,0:T(2,128)} all-reduce(s32[2,64]{1,0:T(2,128)S(1)} %psum.22), channel_id=1, replica_groups=mesh['dp'=4,'ep_0'=4,'ep_1'=8,'ep_2'=2] {'ep_2'}, use_global_device_ids=true, to_apply=%region_15.16 | all-reduce | flops 128 | bytes 1024 | tf_op jit(solution)/shard_map/psum | solution.py:388
  (169 shorter events, 75.8 us)
Async XLA Ops:
  6.7 38.9 %all-to-all-start = ((bf16[64,2,3584]{2,1,0:T(2,128)(2,1)}), bf16[64,2,3584]{2,1,0:T(2,128)(2,1)S(1)}, u32[]{:S(2)}, u32[]{:S(2)}) async-start(bf16[64,2,3584]{2,1,0:T(2,128)(2,1)} %all_to_all.30), calls=%async_computation | async-start | bytes 1835008 | tf_op jit(solution)/shard_map/all_to_all | solution.py:341
  22.6 76.0 %collective-permute-start.12 = (bf16[256,896]{1,0:T(8,128)(2,1)}, bf16[256,896]{1,0:T(8,128)(2,1)S(1)}, u32[]{:S(2)}, u32[]{:S(2)}) collective-permute-start(bf16[256,896]{1,0:T(8,128)(2,1)} %get-tuple-element.14), channel_id=1, source_target_pairs={{0,128},{64,192},{128,0},{192,64},{1,129},{65,193},{129,1},{193,65... | collective-permute-start | bytes 1376264 | tf_op jit(solution)/shard_map/ppermute | solution.py:28
  25.4 74.8 %collective-permute-start.11 = (bf16[256,896]{1,0:T(8,128)(2,1)}, bf16[256,896]{1,0:T(8,128)(2,1)S(1)}, u32[]{:S(2)}, u32[]{:S(2)}) collective-permute-start(bf16[256,896]{1,0:T(8,128)(2,1)} %get-tuple-element.15), channel_id=1, source_target_pairs={{0,192},{64,0},{128,64},{192,128},{1,193},{65,1},{129,65},{193,129... | collective-permute-start | bytes 1376264 | tf_op jit(solution)/shard_map/ppermute | solution.py:28
  26.2 76.3 %collective-permute-start.10 = (bf16[256,896]{1,0:T(8,128)(2,1)}, bf16[256,896]{1,0:T(8,128)(2,1)}, u32[]{:S(2)}, u32[]{:S(2)}) collective-permute-start(bf16[256,896]{1,0:T(8,128)(2,1)} %get-tuple-element.16), channel_id=1, source_target_pairs={{0,64},{64,128},{128,192},{192,0},{1,65},{65,129},{129,193},{193,1... | collective-permute-start | bytes 1376264 | tf_op jit(solution)/shard_map/ppermute | solution.py:28
  46.0 26.6 %collective-permute-start.4 = (bf16[128,3584]{1,0:T(8,128)(2,1)S(1)}, bf16[128,3584]{1,0:T(8,128)(2,1)S(1)}, u32[]{:S(2)}, u32[]{:S(2)}) collective-permute-start(bf16[128,3584]{1,0:T(8,128)(2,1)S(1)} %all_to_all.32.refs_0_), channel_id=1, source_target_pairs={{0,192},{64,0},{128,64},{192,128},{1,193},{65,1},{129,65},{193,129... | collective-permute-start | bytes 2752520 | tf_op jit(solution)/shard_map/ppermute | solution.py:28
  48.5 22.6 %collective-permute-start.3 = (bf16[128,3584]{1,0:T(8,128)(2,1)S(1)}, bf16[128,3584]{1,0:T(8,128)(2,1)S(1)}, u32[]{:S(2)}, u32[]{:S(2)}) collective-permute-start(bf16[128,3584]{1,0:T(8,128)(2,1)S(1)} %all_to_all.32.refs_0_), channel_id=1, source_target_pairs={{0,64},{64,128},{128,192},{192,0},{1,65},{65,129},{129,193},{193,1... | collective-permute-start | bytes 2752520 | tf_op jit(solution)/shard_map/ppermute | solution.py:28
  71.9 20.5 %collective-permute-start.5 = (bf16[128,1792]{1,0:T(8,128)(2,1)}, bf16[128,1792]{1,0:T(8,128)(2,1)}, u32[]{:S(2)}, u32[]{:S(2)}) collective-permute-start(bf16[128,1792]{1,0:T(8,128)(2,1)} %slice.63), channel_id=1, source_target_pairs={{0,64},{64,128},{128,192},{192,0},{1,65},{65,129},{129,193},{193,1... | collective-permute-start | bytes 1376264 | tf_op jit(solution)/shard_map/ppermute | solution.py:28
  72.6 20.9 %collective-permute-start.6 = (bf16[128,1792]{1,0:T(8,128)(2,1)S(1)}, bf16[128,1792]{1,0:T(8,128)(2,1)S(1)}, u32[]{:S(2)}, u32[]{:S(2)}) collective-permute-start(bf16[128,1792]{1,0:T(8,128)(2,1)S(1)} %slice.64), channel_id=1, source_target_pairs={{0,192},{64,0},{128,64},{192,128},{1,193},{65,1},{129,65},{193,129... | collective-permute-start | bytes 1376264 | tf_op jit(solution)/shard_map/ppermute | solution.py:28
  100.2 82.4 %collective-permute-start.27 = (bf16[256,3584]{1,0:T(8,128)(2,1)}, bf16[256,3584]{1,0:T(8,128)(2,1)S(1)}, u32[]{:S(2)}, u32[]{:S(2)}) collective-permute-start(bf16[256,3584]{1,0:T(8,128)(2,1)} %slice_bitcast_fusion), channel_id=1, source_target_pairs={{0,192},{64,0},{128,64},{192,128},{1,193},{65,1},{129,65},{193,129... | collective-permute-start | bytes 5505032 | tf_op jit(solution)/shard_map/ppermute | solution.py:28
  102.5 80.4 %collective-permute-start.26 = (bf16[256,3584]{1,0:T(8,128)(2,1)}, bf16[256,3584]{1,0:T(8,128)(2,1)}, u32[]{:S(2)}, u32[]{:S(2)}) collective-permute-start(bf16[256,3584]{1,0:T(8,128)(2,1)} %slice_bitcast_fusion), channel_id=1, source_target_pairs={{0,64},{64,128},{128,192},{192,0},{1,65},{65,129},{129,193},{193,1... | collective-permute-start | bytes 5505032 | tf_op jit(solution)/shard_map/ppermute | solution.py:28
  105.0 49.1 %collective-permute-start.2 = (bf16[8,1024]{1,0:T(8,128)(2,1)}, bf16[8,1024]{1,0:T(8,128)(2,1)}, u32[]{:S(2)}, u32[]{:S(2)}) collective-permute-start(bf16[8,1024]{1,0:T(8,128)(2,1)} %get-tuple-element.40), channel_id=1, source_target_pairs={{0,128},{64,192},{128,0},{192,64},{1,129},{65,193},{129,1},{193,65... | collective-permute-start | bytes 49160 | tf_op jit(solution)/shard_map/ppermute | solution.py:28
  109.6 43.0 %collective-permute-start = (bf16[8,1024]{1,0:T(8,128)(2,1)}, bf16[8,1024]{1,0:T(8,128)(2,1)}, u32[]{:S(2)}, u32[]{:S(2)}) collective-permute-start(bf16[8,1024]{1,0:T(8,128)(2,1)} %get-tuple-element.41), channel_id=1, source_target_pairs={{0,64},{64,128},{128,192},{192,0},{1,65},{65,129},{129,193},{193,1... | collective-permute-start | bytes 49160 | tf_op jit(solution)/shard_map/ppermute | solution.py:28
  112.7 40.6 %collective-permute-start.1 = (bf16[8,1024]{1,0:T(8,128)(2,1)}, bf16[8,1024]{1,0:T(8,128)(2,1)}, u32[]{:S(2)}, u32[]{:S(2)}) collective-permute-start(bf16[8,1024]{1,0:T(8,128)(2,1)} %get-tuple-element.42), channel_id=1, source_target_pairs={{0,192},{64,0},{128,64},{192,128},{1,193},{65,1},{129,65},{193,129... | collective-permute-start | bytes 49160 | tf_op jit(solution)/shard_map/ppermute | solution.py:28
  116.7 39.8 %all-to-all-start.1 = ((bf16[64,8,896]{2,1,0:T(8,128)(2,1)}), bf16[64,8,896]{2,1,0:T(8,128)(2,1)S(1)}, u32[]{:S(2)}, u32[]{:S(2)}) async-start(bf16[64,8,896]{2,1,0:T(8,128)(2,1)} %bitcast.14), calls=%async_computation.1 | async-start | bytes 1835008 | tf_op jit(solution)/shard_map/all_to_all | solution.py:341
  158.5 53.1 %all-to-all-start.2 = ((bf16[64,8,896]{2,1,0:T(8,128)(2,1)}), bf16[64,8,896]{2,1,0:T(8,128)(2,1)S(1)}, u32[]{:S(2)}, u32[]{:S(2)}) async-start(bf16[64,8,896]{2,1,0:T(8,128)(2,1)} %fusion.6), calls=%async_computation.2 | async-start | bytes 1835008 | tf_op jit(solution)/shard_map/all_to_all | solution.py:341
  168.6 24.1 %collective-permute-start.16 = (bf16[896,256]{1,0:T(8,128)(2,1)}, bf16[896,256]{1,0:T(8,128)(2,1)}, u32[]{:S(2)}, u32[]{:S(2)}) collective-permute-start(bf16[896,256]{1,0:T(8,128)(2,1)} %get-tuple-element.11), channel_id=1, source_target_pairs={{0,64},{64,128},{128,192},{192,0},{1,65},{65,129},{129,193},{193,1... | collective-permute-start | bytes 1376264 | tf_op jit(solution)/shard_map/ppermute | solution.py:28
  168.9 23.7 %collective-permute-start.18 = (bf16[896,256]{1,0:T(8,128)(2,1)}, bf16[896,256]{1,0:T(8,128)(2,1)}, u32[]{:S(2)}, u32[]{:S(2)}) collective-permute-start(bf16[896,256]{1,0:T(8,128)(2,1)} %get-tuple-element.13), channel_id=1, source_target_pairs={{0,192},{64,0},{128,64},{192,128},{1,193},{65,1},{129,65},{193,129... | collective-permute-start | bytes 1376264 | tf_op jit(solution)/shard_map/ppermute | solution.py:28
  182.0 19.0 %collective-permute-start.21 = (bf16[896,256]{1,0:T(8,128)(2,1)}, bf16[896,256]{1,0:T(8,128)(2,1)}, u32[]{:S(2)}, u32[]{:S(2)}) collective-permute-start(bf16[896,256]{1,0:T(8,128)(2,1)} %get-tuple-element.6), channel_id=1, source_target_pairs={{0,128},{64,192},{128,0},{192,64},{1,129},{65,193},{129,1},{193,65... | collective-permute-start | bytes 1376264 | tf_op jit(solution)/shard_map/ppermute | solution.py:28
  182.6 29.0 %collective-permute-start.17 = (bf16[896,256]{1,0:T(8,128)(2,1)}, bf16[896,256]{1,0:T(8,128)(2,1)}, u32[]{:S(2)}, u32[]{:S(2)}) collective-permute-start(bf16[896,256]{1,0:T(8,128)(2,1)} %get-tuple-element.7), channel_id=1, source_target_pairs={{0,64},{64,128},{128,192},{192,0},{1,65},{65,129},{129,193},{193,1... | collective-permute-start | bytes 1376264 | tf_op jit(solution)/shard_map/ppermute | solution.py:28
  182.9 28.7 %collective-permute-start.19 = (bf16[896,256]{1,0:T(8,128)(2,1)}, bf16[896,256]{1,0:T(8,128)(2,1)}, u32[]{:S(2)}, u32[]{:S(2)}) collective-permute-start(bf16[896,256]{1,0:T(8,128)(2,1)} %get-tuple-element.9), channel_id=1, source_target_pairs={{0,192},{64,0},{128,64},{192,128},{1,193},{65,1},{129,65},{193,129... | collective-permute-start | bytes 1376264 | tf_op jit(solution)/shard_map/ppermute | solution.py:28
  192.7 47.5 %collective-permute-start.29 = (bf16[128,3584]{1,0:T(8,128)(2,1)}, bf16[128,3584]{1,0:T(8,128)(2,1)}, u32[]{:S(2)}, u32[]{:S(2)}) collective-permute-start(bf16[128,3584]{1,0:T(8,128)(2,1)} %slice.69), channel_id=1, source_target_pairs={{0,192},{64,0},{128,64},{192,128},{1,193},{65,1},{129,65},{193,129... | collective-permute-start | bytes 2752520 | tf_op jit(solution)/shard_map/ppermute | solution.py:28
  192.7 47.5 %collective-permute-start.28 = (bf16[128,3584]{1,0:T(8,128)(2,1)}, bf16[128,3584]{1,0:T(8,128)(2,1)}, u32[]{:S(2)}, u32[]{:S(2)}) collective-permute-start(bf16[128,3584]{1,0:T(8,128)(2,1)} %slice.68), channel_id=1, source_target_pairs={{0,64},{64,128},{128,192},{192,0},{1,65},{65,129},{129,193},{193,1... | collective-permute-start | bytes 2752520 | tf_op jit(solution)/shard_map/ppermute | solution.py:28
  258.2 48.3 %all-to-all-start.3 = ((bf16[64,2,3584]{2,1,0:T(2,128)(2,1)}), bf16[64,2,3584]{2,1,0:T(2,128)(2,1)S(1)}, u32[]{:S(2)}, u32[]{:S(2)}) async-start(bf16[64,2,3584]{2,1,0:T(2,128)(2,1)} %all_to_all.39), calls=%async_computation.3 | async-start | bytes 1835008 | tf_op jit(solution)/shard_map/all_to_all | solution.py:341
  270.0 34.4 %collective-permute-start.13 = (bf16[8,896]{1,0:T(8,128)(2,1)S(1)}, bf16[8,896]{1,0:T(8,128)(2,1)S(1)}, u32[]{:S(2)}, u32[]{:S(2)}) collective-permute-start(bf16[8,896]{1,0:T(8,128)(2,1)S(1)} %get-tuple-element.22), channel_id=1, source_target_pairs={{0,64},{64,128},{128,192},{192,0},{1,65},{65,129},{129,193},{193,1... | collective-permute-start | bytes 43016 | tf_op jit(solution)/shard_map/ppermute | solution.py:28
  (29 other events, 369.6 us)
